TPU v7x, 32 devices: a whole 2x2x4 slice. The times are simulated.
32 devices in a mesh: pp: 2 (over core), ep: 16 (over z, y, x), tp: 1.
Axes of the slice: x: 2, y: 2, z: 4, core: 2. Of those that a mesh axis runs over, the one named last changes fastest.
Arguments:
- acts: bfloat16 [2, 96, 3072], P(None, 'ep'), may hold values from -6 to 6
- route_ids: int32 [2, 2, 96, 8], P('pp', None, 'ep'), may hold values from 0 to 23, all different within a row; in each aligned block of 6 rows (0 to 5, 6 to 11, ..., all dimensions but the last counted through in order) at most 2 rows name the same one
- norm_gain: bfloat16 [2, 3072], P('pp'), may hold values from 0.5 to 1.5
- router: bfloat16 [2, 3072, 24], P('pp'), may hold values from -0.109375 to 0.109375
- dense_gate: bfloat16 [2, 3072, 6144], P('pp', None, ('ep', 'tp')), may hold values from -0.109375 to 0.109375
- dense_up: bfloat16 [2, 3072, 6144], P('pp', None, ('ep', 'tp')), may hold values from -0.109375 to 0.109375
- dense_down: bfloat16 [2, 6144, 3072], P('pp', ('ep', 'tp')), may hold values from -0.078125 to 0.078125
- expert_gate: bfloat16 [2, 16, 3072, 1024], P('pp', 'ep', None, 'tp'), may hold values from -0.109375 to 0.109375
- expert_up: bfloat16 [2, 16, 3072, 1024], P('pp', 'ep', None, 'tp'), may hold values from -0.109375 to 0.109375
- expert_down: bfloat16 [2, 16, 1024, 3072], P('pp', 'ep', 'tp'), may hold values from -0.1875 to 0.1875
Outputs:
- layer_out: bfloat16 [2, 2, 96, 3072], P('pp', None, 'ep')
Inputs may be any that keep to these rules, and one draw needn't show every extreme that they name: `route_ids`: the 8 ids of a token differ. In each layer and microbatch, among the 6 tokens of one ep index no id is named by more than 2 tokens, a bound that some block reaches.
All inputs are finite; a program needn't handle non-finite values.
Results may differ from a plain program's by a relative error of at most 0.008.
Values may be sent and summed in bfloat16 or wider, within the bound.
A program may use at most 128 MiB of HBM per device.

v0:
```python
import jax
import jax.numpy as jnp
from jax import lax
from jax.sharding import PartitionSpec as P


def from_behind(block, axis, distance):
    devices = range(lax.axis_size(axis))
    route = [(i - distance, i) for i in devices if i - distance in devices]
    return lax.ppermute(block, axis, route)


def normalize(inputs, gain):
    widened = inputs.astype(jnp.float32)
    spread = jnp.mean(widened * widened, axis=-1, keepdims=True)
    normed = (widened * lax.rsqrt(spread + 1e-06) * gain.astype(jnp.float32)).astype(jnp.bfloat16)
    return (widened, normed)


def gated_block(inputs, w_gate, w_up, w_down):
    gate_part = jnp.dot(inputs, w_gate, preferred_element_type=jnp.float32)
    up_part = jnp.dot(inputs, w_up, preferred_element_type=jnp.float32)
    hidden = (jax.nn.silu(gate_part) * up_part).astype(jnp.bfloat16)
    return jnp.dot(hidden, w_down, preferred_element_type=jnp.float32)


def choice_weights(normed, route_rows, router_w, n_real):
    n_total = router_w.shape[1]
    gates = jax.nn.sigmoid(jnp.dot(normed, router_w, preferred_element_type=jnp.float32))
    picked = (route_rows[:, :, None] == jnp.arange(n_total, dtype=jnp.int32)[None, None, :]).astype(
        jnp.float32
    )
    weights = jnp.sum(picked * gates[:, None, :], axis=-1)
    zero_share = jnp.sum(jnp.where(route_rows >= n_real, weights, jnp.float32(0.0)), axis=-1)
    return (weights, picked, zero_share)


def on_device(
    acts,
    route_ids,
    norm_gain,
    router,
    dense_gate,
    dense_up,
    dense_down,
    expert_gate,
    expert_up,
    expert_down,
):
    n_micro, per_group, width = acts.shape
    top_count = route_ids.shape[-1]
    n_groups = lax.axis_size("ep")
    n_pairs = lax.axis_size("tp")
    section = lax.axis_index("pp")
    group_pos = lax.axis_index("ep")
    pair_pos = lax.axis_index("tp")
    micro_rows = per_group * n_groups
    share = per_group // n_pairs
    gain = norm_gain[0]
    router_w = router[0]
    total_ids = router_w.shape[1]
    slot_count = max(2, (per_group * top_count + total_ids - 1) // total_ids)
    d_gate = dense_gate[0]
    d_up = dense_up[0]
    d_down = dense_down[0]
    e_gate = expert_gate[0, 0]
    e_up = expert_up[0, 0]
    e_down = expert_down[0, 0]
    slot_range = jnp.arange(slot_count, dtype=jnp.float32)
    incoming = jnp.zeros((per_group, width), jnp.bfloat16)
    outputs = jnp.zeros((n_micro, per_group, width), jnp.bfloat16)
    for tick_index in range(n_micro + 1):
        local_micro = tick_index - section
        micro_index = jnp.clip(local_micro, 0, n_micro - 1)
        valid = jnp.logical_and(local_micro >= 0, local_micro < n_micro)
        first_input = acts[min(tick_index, n_micro - 1)]
        current = jnp.where(section == 0, first_input, incoming)
        route_rows = lax.dynamic_index_in_dim(route_ids[0], micro_index, 0, keepdims=False)
        widened, normed = normalize(current, gain)
        weights, picked, zero_share = choice_weights(normed, route_rows, router_w, n_groups)
        all_normed = lax.all_gather(normed, "ep", axis=0, tiled=True)
        real_pick = picked[:, :, :n_groups]
        hot = jnp.sum(real_pick, axis=1)
        coef = jnp.einsum("tk,tke->te", weights, real_pick, precision=lax.Precision.HIGHEST)
        position = jnp.cumsum(hot, axis=0) - hot
        select = hot.T[:, None, :] * (position.T[:, None, :] == slot_range[None, :, None]).astype(
            jnp.float32
        )
        outgoing = jnp.einsum(
            "esi,id->esd", select.astype(jnp.bfloat16), normed, preferred_element_type=jnp.float32
        ).astype(jnp.bfloat16)
        received = lax.all_to_all(outgoing, "ep", split_axis=0, concat_axis=0, tiled=True)
        flat = received.reshape(-1, width)
        produced = gated_block(flat, e_gate, e_up, e_down).reshape(received.shape[:-1] + (width,))
        returned = lax.all_to_all(produced, "ep", split_axis=0, concat_axis=0, tiled=True)
        own_rows = jnp.einsum(
            "esi,esd->id", select * coef.T[:, None, :], returned, precision=lax.Precision.HIGHEST
        )
        extra = lax.dynamic_update_slice_in_dim(
            jnp.zeros((micro_rows, width), jnp.float32), own_rows, group_pos * per_group, 0
        )
        summed = lax.psum_scatter(
            gated_block(all_normed, d_gate, d_up, d_down) + extra,
            ("ep", "tp"),
            scatter_dimension=0,
            tiled=True,
        )
        offset = pair_pos * share
        own_inputs = lax.dynamic_slice_in_dim(widened, offset, share, 0)
        own_normed = lax.dynamic_slice_in_dim(normed, offset, share, 0).astype(jnp.float32)
        own_zero = lax.dynamic_slice_in_dim(zero_share, offset, share, 0)
        result_part = (own_inputs + summed + own_zero[:, None] * own_normed).astype(jnp.bfloat16)
        finished = lax.all_gather(result_part, "tp", axis=0, tiled=True)
        updated = lax.dynamic_update_index_in_dim(outputs, finished, micro_index, 0)
        outputs = jnp.where(valid, updated, outputs)
        if tick_index < n_micro:
            incoming = from_behind(finished, "pp", 1)
    return outputs[None]


def solution(mesh):
    return jax.shard_map(
        on_device,
        mesh=mesh,
        in_specs=(
            P(None, "ep", None),
            P("pp", None, "ep", None),
            P("pp", None),
            P("pp", None, None),
            P("pp", None, ("ep", "tp")),
            P("pp", None, ("ep", "tp")),
            P("pp", ("ep", "tp"), None),
            P("pp", "ep", None, "tp"),
            P("pp", "ep", None, "tp"),
            P("pp", "ep", "tp", None),
        ),
        out_specs=P("pp", None, "ep", None),
        check_vma=False,
    )
```

profile of v0, /device:TPU:0, one launch (start us, length us, event | category | flops | bytes accessed | tf_op | source)
XLA Modules:
  0.0 461.7 jit_solution(911177788010176452)
XLA Ops:
  4.8 8.3 %all-to-all-start = ((bf16[16,2,3072]{2,1,0:T(2,128)(2,1)}), bf16[16,2,3072]{2,1,0:T(2,128)(2,1)S(1)}, u32[]{:S(2)}, u32[]{:S(2)}) async-start(bf16[16,2,3072]{2,1,0:T(2,128)(2,1)} %copy.46), calls=%async_computation | async-start | bytes 393216 | tf_op jit(solution)/shard_map/all_to_all | solution.py:92
  15.1 48.1 %all-gather = bf16[16,6,3072]{2,1,0:T(8,128)(2,1)} all-gather(bf16[1,6,3072]{2,1,0:T(8,128)(2,1)S(1)} %fusion.192), channel_id=1, replica_groups=mesh['pp'=2,'ep'=16,'tp'=1] {'ep'}, dimensions={0}, use_global_device_ids=true | all-gather | bytes 626688 | tf_op jit(solution)/shard_map/all_gather | solution.py:81
  63.3 4.1 fusion.19
  69.2 4.0 fusion.7
  74.2 3.6 all-to-all-start.1
  81.0 2.9 fusion.40
  83.9 3.8 fusion.28
  90.7 50.0 %fusion = f32[8,3072]{1,0:T(8,128)S(1)} fusion(f32[96,3072]{1,0:T(8,128)} %add.116), kind=kCustom, calls=%all-reduce-scatter | all-reduce-scatter fusion | flops 393217 | bytes 1278464
  143.8 5.1 %collective-permute-start.4 = (f32[8,3072]{1,0:T(8,128)S(1)}, f32[8,3072]{1,0:T(8,128)S(1)}, u32[]{:S(2)}, u32[]{:S(2)}) collective-permute-start(f32[8,3072]{1,0:T(8,128)S(1)} %fusion), channel_id=1, source_target_pairs={{0,3},{1,4},{2,5},{3,6},{4,7},{5,8},{6,9},{7,10},{8,11},{9,12},{10... | collective-permute-start | bytes 294920
  148.9 3.3 collective-permute-start.5
  161.3 4.7 %all-to-all-start.2 = ((bf16[16,2,3072]{2,1,0:T(2,128)(2,1)}), bf16[16,2,3072]{2,1,0:T(2,128)(2,1)S(1)}, u32[]{:S(2)}, u32[]{:S(2)}) async-start(bf16[16,2,3072]{2,1,0:T(2,128)(2,1)} %copy.52), calls=%async_computation.2 | async-start | bytes 393216 | tf_op jit(solution)/shard_map/all_to_all | solution.py:92
  166.1 48.3 %all-gather.1 = bf16[16,6,3072]{2,1,0:T(8,128)(2,1)} all-gather(bf16[1,6,3072]{2,1,0:T(8,128)(2,1)S(1)} %fusion.198), channel_id=1, replica_groups=mesh['pp'=2,'ep'=16,'tp'=1] {'ep'}, dimensions={0}, use_global_device_ids=true | all-gather | bytes 626688 | tf_op jit(solution)/shard_map/all_gather | solution.py:81
  214.5 4.0 fusion.17
  218.5 4.0 fusion.72
  222.5 4.0 fusion.5
  227.5 3.7 all-to-all-start.3
  232.8 2.8 fusion.38
  235.6 3.8 fusion.26
  243.9 49.4 %fusion.1 = f32[8,3072]{1,0:T(8,128)S(1)} fusion(f32[96,3072]{1,0:T(8,128)} %add.123), kind=kCustom, calls=%all-reduce-scatter.1 | all-reduce-scatter fusion | flops 393217 | bytes 1278464
  295.9 4.6 collective-permute-start.8
  300.5 2.8 collective-permute-start.9
  313.3 5.3 %all-to-all-start.4 = ((bf16[16,2,3072]{2,1,0:T(2,128)(2,1)}), bf16[16,2,3072]{2,1,0:T(2,128)(2,1)S(1)}, u32[]{:S(2)}, u32[]{:S(2)}) async-start(bf16[16,2,3072]{2,1,0:T(2,128)(2,1)} %copy.57), calls=%async_computation.4 | async-start | bytes 393216 | tf_op jit(solution)/shard_map/all_to_all | solution.py:92
  318.8 48.3 %all-gather.2 = bf16[16,6,3072]{2,1,0:T(8,128)(2,1)} all-gather(bf16[1,6,3072]{2,1,0:T(8,128)(2,1)S(1)} %fusion.195), channel_id=1, replica_groups=mesh['pp'=2,'ep'=16,'tp'=1] {'ep'}, dimensions={0}, use_global_device_ids=true | all-gather | bytes 626688 | tf_op jit(solution)/shard_map/all_gather | solution.py:81
  367.1 4.0 fusion.15
  371.1 4.0 fusion.69
  375.1 4.0 fusion.3
  380.2 3.6 all-to-all-start.5
  385.2 2.9 fusion.36
  388.1 3.8 fusion.24
  396.3 49.4 %fusion.2 = f32[8,3072]{1,0:T(8,128)S(1)} fusion(f32[96,3072]{1,0:T(8,128)} %add.130), kind=kCustom, calls=%all-reduce-scatter.2 | all-reduce-scatter fusion | flops 393217 | bytes 1278464
  448.3 4.6 collective-permute-start.12
  452.9 2.7 collective-permute-start.13
  (133 shorter events, 63.0 us)
Async XLA Ops:
  0.0 83.9 %copy-start = (bf16[1,384,3072]{2,1,0:T(8,128)(2,1)S(1)}, bf16[1,384,3072]{2,1,0:T(8,128)(2,1)}, u32[]{:S(2)}) copy-start(bf16[1,384,3072]{2,1,0:T(8,128)(2,1)} %param.16) | copy-start | bytes 7077892
  2.9 10.3 %copy-start.9 = (f32[6]{0:T(128)}, f32[6]{0:T(128)S(1)}, u32[]{:S(2)}) copy-start(f32[6]{0:T(128)S(1)} %add_rsqrt_fusion.2) | copy-start | bytes 76
  4.8 58.4 %all-to-all-start = ((bf16[16,2,3072]{2,1,0:T(2,128)(2,1)}), bf16[16,2,3072]{2,1,0:T(2,128)(2,1)S(1)}, u32[]{:S(2)}, u32[]{:S(2)}) async-start(bf16[16,2,3072]{2,1,0:T(2,128)(2,1)} %copy.46), calls=%async_computation | async-start | bytes 393216 | tf_op jit(solution)/shard_map/all_to_all | solution.py:92
  63.3 4.6 copy-start.1
  73.1 6.7 %copy-start.12 = (u32[32]{0:T(128)S(1)}, u32[32]{0:T(128)}, u32[]{:S(2)}) copy-start(u32[32]{0:T(128)} %constant.91) | copy-start | bytes 388
  74.2 13.5 %all-to-all-start.1 = ((f32[16,2,3072]{2,1,0:T(2,128)}), f32[16,2,3072]{2,1,0:T(2,128)S(1)}, u32[]{:S(2)}, u32[]{:S(2)}) async-start(f32[16,2,3072]{2,1,0:T(2,128)} %copy.48), calls=%async_computation.1 | async-start | bytes 786432 | tf_op jit(solution)/shard_map/all_to_all | solution.py:95
  140.7 13.7 %collective-permute-start.2 = (f32[8,3072]{1,0:T(8,128)S(1)}, f32[8,3072]{1,0:T(8,128)S(1)}, u32[]{:S(2)}, u32[]{:S(2)}) collective-permute-start(f32[8,3072]{1,0:T(8,128)S(1)} %fusion), channel_id=1, source_target_pairs={{0,1},{1,2},{2,3},{3,4},{4,5},{5,6},{6,7},{7,8},{8,9},{9,10},{10,1... | collective-permute-start | bytes 294920
  142.5 11.9 %collective-permute-start.3 = (f32[8,3072]{1,0:T(8,128)S(1)}, f32[8,3072]{1,0:T(8,128)S(1)}, u32[]{:S(2)}, u32[]{:S(2)}) collective-permute-start(f32[8,3072]{1,0:T(8,128)S(1)} %fusion), channel_id=1, source_target_pairs={{0,2},{1,3},{2,4},{3,5},{4,6},{5,7},{6,8},{7,9},{8,10},{9,11},{10,... | collective-permute-start | bytes 294920
  143.8 10.6 %collective-permute-start.4 = (f32[8,3072]{1,0:T(8,128)S(1)}, f32[8,3072]{1,0:T(8,128)S(1)}, u32[]{:S(2)}, u32[]{:S(2)}) collective-permute-start(f32[8,3072]{1,0:T(8,128)S(1)} %fusion), channel_id=1, source_target_pairs={{0,3},{1,4},{2,5},{3,6},{4,7},{5,8},{6,9},{7,10},{8,11},{9,12},{10... | collective-permute-start | bytes 294920
  148.9 5.5 %collective-permute-start.5 = (f32[6,3072]{1,0:T(8,128)S(1)}, f32[6,3072]{1,0:T(8,128)S(1)}, u32[]{:S(2)}, u32[]{:S(2)}) collective-permute-start(f32[6,3072]{1,0:T(8,128)S(1)} %slice.36), channel_id=1, source_target_pairs={{0,4},{1,5},{2,6},{3,7},{4,8},{5,9},{6,10},{7,11},{8,12},{9,13},{1... | collective-permute-start | bytes 221192
  155.7 2.2 collective-permute-start
  158.9 2.4 copy-start.10
  161.3 53.1 %all-to-all-start.2 = ((bf16[16,2,3072]{2,1,0:T(2,128)(2,1)}), bf16[16,2,3072]{2,1,0:T(2,128)(2,1)S(1)}, u32[]{:S(2)}, u32[]{:S(2)}) async-start(bf16[16,2,3072]{2,1,0:T(2,128)(2,1)} %copy.52), calls=%async_computation.2 | async-start | bytes 393216 | tf_op jit(solution)/shard_map/all_to_all | solution.py:92
  166.1 65.1 %copy-start.7 = (f32[6,8]{1,0:T(8,128)}, f32[6,8]{1,0:T(8,128)S(1)}, u32[]{:S(2)}) copy-start(f32[6,8]{1,0:T(8,128)S(1)} %select_reduce_fusion.1) | copy-start | bytes 580
  227.5 13.3 %all-to-all-start.3 = ((f32[16,2,3072]{2,1,0:T(2,128)}), f32[16,2,3072]{2,1,0:T(2,128)S(1)}, u32[]{:S(2)}, u32[]{:S(2)}) async-start(f32[16,2,3072]{2,1,0:T(2,128)} %copy.54), calls=%async_computation.3 | async-start | bytes 786432 | tf_op jit(solution)/shard_map/all_to_all | solution.py:95
  235.6 67.6 %copy-start.8 = (f32[6,8]{1,0:T(8,128)S(1)}, f32[6,8]{1,0:T(8,128)}, u32[]{:S(2)}) copy-start(f32[6,8]{1,0:T(8,128)} %copy-done.7) | copy-start | bytes 580
  239.5 69.0 %copy-start.11 = (f32[6]{0:T(128)S(1)}, f32[6]{0:T(128)}, u32[]{:S(2)}) copy-start(f32[6]{0:T(128)} %copy-done.10) | copy-start | bytes 76
  242.2 68.5 %copy-start.2 = (bf16[1,6,3072]{2,0,1:T(2,128)(2,1)S(1)}, bf16[1,6,3072]{2,0,1:T(2,128)(2,1)}, u32[]{:S(2)}) copy-start(bf16[1,6,3072]{2,0,1:T(2,128)(2,1)} %get-tuple-element.15) | copy-start | bytes 110596
  293.3 12.2 %collective-permute-start.6 = (f32[8,3072]{1,0:T(8,128)S(1)}, f32[8,3072]{1,0:T(8,128)S(1)}, u32[]{:S(2)}, u32[]{:S(2)}) collective-permute-start(f32[8,3072]{1,0:T(8,128)S(1)} %fusion.1), channel_id=1, source_target_pairs={{0,1},{1,2},{2,3},{3,4},{4,5},{5,6},{6,7},{7,8},{8,9},{9,10},{10,1... | collective-permute-start | bytes 294920
  294.6 10.9 %collective-permute-start.7 = (f32[8,3072]{1,0:T(8,128)S(1)}, f32[8,3072]{1,0:T(8,128)S(1)}, u32[]{:S(2)}, u32[]{:S(2)}) collective-permute-start(f32[8,3072]{1,0:T(8,128)S(1)} %fusion.1), channel_id=1, source_target_pairs={{0,2},{1,3},{2,4},{3,5},{4,6},{5,7},{6,8},{7,9},{8,10},{9,11},{10,... | collective-permute-start | bytes 294920
  295.9 10.2 %collective-permute-start.8 = (f32[8,3072]{1,0:T(8,128)S(1)}, f32[8,3072]{1,0:T(8,128)}, u32[]{:S(2)}, u32[]{:S(2)}) collective-permute-start(f32[8,3072]{1,0:T(8,128)S(1)} %fusion.1), channel_id=1, source_target_pairs={{0,3},{1,4},{2,5},{3,6},{4,7},{5,8},{6,9},{7,10},{8,11},{9,12},{10... | collective-permute-start | bytes 294920
  300.5 5.0 %collective-permute-start.9 = (f32[6,3072]{1,0:T(8,128)S(1)}, f32[6,3072]{1,0:T(8,128)S(1)}, u32[]{:S(2)}, u32[]{:S(2)}) collective-permute-start(f32[6,3072]{1,0:T(8,128)S(1)} %slice.37), channel_id=1, source_target_pairs={{0,4},{1,5},{2,6},{3,7},{4,8},{5,9},{6,10},{7,11},{8,12},{9,13},{1... | collective-permute-start | bytes 221192
  305.4 0.6 copy-start.4
  308.6 2.2 collective-permute-start.1
  313.3 53.8 %all-to-all-start.4 = ((bf16[16,2,3072]{2,1,0:T(2,128)(2,1)}), bf16[16,2,3072]{2,1,0:T(2,128)(2,1)S(1)}, u32[]{:S(2)}, u32[]{:S(2)}) async-start(bf16[16,2,3072]{2,1,0:T(2,128)(2,1)} %copy.57), calls=%async_computation.4 | async-start | bytes 393216 | tf_op jit(solution)/shard_map/all_to_all | solution.py:92
  380.2 13.2 %all-to-all-start.5 = ((f32[16,2,3072]{2,1,0:T(2,128)}), f32[16,2,3072]{2,1,0:T(2,128)S(1)}, u32[]{:S(2)}, u32[]{:S(2)}) async-start(f32[16,2,3072]{2,1,0:T(2,128)} %copy.59), calls=%async_computation.5 | async-start | bytes 786432 | tf_op jit(solution)/shard_map/all_to_all | solution.py:95
  394.7 66.2 %copy-start.3 = (bf16[1,2,6,3072]{3,2,1,0:T(8,128)(2,1)S(1)}, bf16[1,2,6,3072]{3,2,1,0:T(8,128)(2,1)}, u32[]{:S(2)}) copy-start(bf16[1,2,6,3072]{3,2,1,0:T(8,128)(2,1)} %copy.121) | copy-start | bytes 221188
  445.7 12.1 %collective-permute-start.10 = (f32[8,3072]{1,0:T(8,128)S(1)}, f32[8,3072]{1,0:T(8,128)S(1)}, u32[]{:S(2)}, u32[]{:S(2)}) collective-permute-start(f32[8,3072]{1,0:T(8,128)S(1)} %fusion.2), channel_id=1, source_target_pairs={{0,1},{1,2},{2,3},{3,4},{4,5},{5,6},{6,7},{7,8},{8,9},{9,10},{10,1... | collective-permute-start | bytes 294920
  447.0 10.8 %collective-permute-start.11 = (f32[8,3072]{1,0:T(8,128)S(1)}, f32[8,3072]{1,0:T(8,128)S(1)}, u32[]{:S(2)}, u32[]{:S(2)}) collective-permute-start(f32[8,3072]{1,0:T(8,128)S(1)} %fusion.2), channel_id=1, source_target_pairs={{0,2},{1,3},{2,4},{3,5},{4,6},{5,7},{6,8},{7,9},{8,10},{9,11},{10,... | collective-permute-start | bytes 294920
  448.3 10.2 %collective-permute-start.12 = (f32[8,3072]{1,0:T(8,128)S(1)}, f32[8,3072]{1,0:T(8,128)}, u32[]{:S(2)}, u32[]{:S(2)}) collective-permute-start(f32[8,3072]{1,0:T(8,128)S(1)} %fusion.2), channel_id=1, source_target_pairs={{0,3},{1,4},{2,5},{3,6},{4,7},{5,8},{6,9},{7,10},{8,11},{9,12},{10... | collective-permute-start | bytes 294920
  452.9 4.9 %collective-permute-start.13 = (f32[6,3072]{1,0:T(8,128)S(1)}, f32[6,3072]{1,0:T(8,128)S(1)}, u32[]{:S(2)}, u32[]{:S(2)}) collective-permute-start(f32[6,3072]{1,0:T(8,128)S(1)} %slice.38), channel_id=1, source_target_pairs={{0,4},{1,5},{2,6},{3,7},{4,8},{5,9},{6,10},{7,11},{8,12},{9,13},{1... | collective-permute-start | bytes 221192
  457.8 0.6 copy-start.5
  (1 other events, 0.6 us)
where the time goes:
time: 464 us; the launch traced here: 462 us
  blocking collectives  293 us (63%)
  starting transfers between devices  63.1 us (14%)
  matrix products  61.8 us (13%)
  local copies, waits for them, and re-layouts  27.9 us (6%)
  waiting for transfers between devices  9.39 us (2%)
  other arithmetic  5.04 us (1%)
    unnamed x3, blocking collectives  149 us
    all_gather x3, blocking collectives, on_device(): all_normed = lax.all_gather(normed, 'ep', axis=0, tiled=True)  145 us
    unnamed x12, starting transfers between devices  31.3 us
    dot_general x6, matrix products, gated_block(): return jnp.dot(hidden, w_down, preferred_element_type=jnp.float32)  23.4 us
    dot_general x6, matrix products, gated_block(): gate_part = jnp.dot(inputs, w_gate, preferred_element_type=jnp.float32)  20.6 us
    all_to_all x3, starting transfers between devices, on_device(): lax.all_to_all(outgoing, 'ep', split_axis=0, concat_axis=0, tiled=True)  18.3 us
    unnamed x38, local copies, waits for them, and re-layouts  12.9 us
    all_to_all x3, starting transfers between devices, on_device(): lax.all_to_all(produced, 'ep', split_axis=0, concat_axis=0, tiled=True)  10.8 us
  transfers between devices with their start and end apart: 20, of which 7 were waited for; matrix products, arithmetic and copies ran while one was open for 6% of the time, Pallas kernels for 0%

commit v1 on v0

v1 whole, which is shorter than its diff:
```python
import functools

import jax
import jax.numpy as jnp
from jax import lax
from jax.experimental import pallas as pl
from jax.experimental.pallas import tpu as pltpu
from jax.sharding import PartitionSpec as P

MESH = pl.DeviceIdType.MESH
F32 = jnp.float32
BF16 = jnp.bfloat16


def divisor_at_most(size, unit, limit):
    best = size
    for step in range(unit, size + 1, unit):
        if size % step == 0 and step <= limit:
            best = step
    return best


class Plan:
    def __init__(self, n_pp, n_ep, n_tp, rows, width, f_expert, f_dense):
        self.n_pp, self.n_ep, self.n_tp = n_pp, n_ep, n_tp
        self.planes = 4 if n_ep % 4 == 0 else 1
        self.depth = n_ep // self.planes
        self.rows = rows
        self.padded = -(-rows // 16) * 16
        self.width = width
        self.total = n_ep * rows
        self.column = self.depth * rows
        self.f_expert, self.f_dense = f_expert, f_dense
        self.n_pieces = 2 if width % 256 == 0 else 1
        self.piece = width // self.n_pieces
        self.n_out = divisor_at_most(self.piece, 128, 512)
        self.chunks = width // self.n_out
        self.per_piece = self.piece // self.n_out
        self.e_step = divisor_at_most(f_expert, 128, 256)
        self.batch = 4 if n_ep % 4 == 0 else 1
        self.peers = self.planes * n_tp - 1


def main_kernel(p, x_ref, hot_ref, gain_ref, router_ref, dg_hbm, du_hbm, dd_hbm, eg_hbm, eu_hbm, ed_hbm,
                out_ref, x_all, hot_all, normed, hot_rows, stage, dg, du, dd, eg, eu, ed, hid_d, hid_e,
                part, recv1, s2, recv2, colf, own_normed, w_sem, x_send, x_fwd, x_recv, h_send, h_fwd, h_recv,
                r1_send, r1_recv, r2_send, r2_recv):
    section = lax.axis_index("pp")
    ep = lax.axis_index("ep")
    tp = lax.axis_index("tp")
    z = ep // p.planes
    q = ep % p.planes
    mine = q * p.depth + z

    loads = {}
    order = [("dg", dg_hbm, dg), ("du", du_hbm, du)]
    for j in range(p.f_expert // p.e_step):
        cols = pl.ds(j * p.e_step, p.e_step)
        order.append((("eg", j), eg_hbm.at[:, cols], eg.at[:, cols]))
        order.append((("eu", j), eu_hbm.at[:, cols], eu.at[:, cols]))
    for c in range(p.chunks):
        cols = pl.ds(c * p.n_out, p.n_out)
        order.append((("dd", c), dd_hbm.at[:, cols], dd.at[:, cols]))
        order.append((("ed", c), ed_hbm.at[:, cols], ed.at[:, cols]))
    for i, (name, src, dst) in enumerate(order):
        loads[name] = pltpu.make_async_copy(src, dst, w_sem.at[i])
        loads[name].start()

    def z_peer(i):
        return lax.rem(z + i, p.depth) * p.planes + q

    def plane_peer(i):
        return z * p.planes + lax.rem(q + i, p.planes)

    barrier = pltpu.get_barrier_semaphore()
    greeted = 0
    for ds in range(p.n_pp):
        for dt in range(p.n_tp):
            targets = [z_peer(i) for i in range(1, p.depth)] if dt == 0 else []
            targets += [plane_peer(i) for i in range(1 if ds == 0 and dt == 0 else 0, p.planes)]
            for target in targets:
                pl.semaphore_signal(
                    barrier, inc=1,
                    device_id={"pp": lax.rem(section + ds, p.n_pp), "ep": target, "tp": lax.rem(tp + dt, p.n_tp)},
                    device_id_type=MESH)
                greeted += 1
    pl.semaphore_wait(barrier, greeted)

    def send(src, dst, send_sem, recv_sem, to_section, to_ep, to_tp):
        pltpu.make_async_remote_copy(
            src_ref=src, dst_ref=dst, send_sem=send_sem, recv_sem=recv_sem,
            device_id={"pp": to_section, "ep": to_ep, "tp": to_tp}, device_id_type=MESH).start()

    def arrived(ref, sem):
        pltpu.make_async_copy(ref, ref, sem).wait()

    def scatter_block(src, buf, send_sem, recv_sem, to_section, include_self):
        for i in range(1, p.depth):
            send(src, buf.at[mine], send_sem, recv_sem.at[mine], to_section, z_peer(i), tp)
        for i in range(0 if include_self else 1, p.planes):
            send(src, buf.at[mine], send_sem, recv_sem.at[mine], to_section, plane_peer(i), tp)

    def forward_blocks(buf, fwd_sem, recv_sem):
        for i in range(1, p.depth):
            block = q * p.depth + lax.rem(z + i, p.depth)
            arrived(buf.at[block], recv_sem.at[block])
            for k in range(1, p.planes):
                send(buf.at[block], buf.at[block], fwd_sem, recv_sem.at[block], section, plane_peer(k), tp)

    def collect_blocks(buf, recv_sem):
        for k in range(1, p.planes):
            column = lax.rem(q + k, p.planes)
            for i in range(p.depth):
                block = column * p.depth + i
                arrived(buf.at[block], recv_sem.at[block])

    n_own = p.depth - 1 + p.planes - 1
    n_fwd = (p.depth - 1) * (p.planes - 1)

    @pl.when(section == 0)
    def _():
        for a in range(p.n_pieces):
            scatter_block(x_ref.at[a], x_all.at[a], x_send.at[a], x_recv.at[a], section, False)
            x_all[a, mine] = x_ref[a]

    scatter_block(hot_ref, hot_all, h_send, h_recv, section, False)
    hot_all[mine] = hot_ref[...]
    s2[...] = jnp.zeros_like(s2)

    @pl.when(section == 0)
    def _():
        for a in range(p.n_pieces):
            forward_blocks(x_all.at[a], x_fwd.at[a], x_recv.at[a])

    forward_blocks(hot_all, h_fwd, h_recv)
    collect_blocks(hot_all, h_recv)

    @pl.when(section > 0)
    def _():
        for a in range(p.n_pieces):
            arrived(x_all.at[a, mine], x_recv.at[a, mine])
            forward_blocks(x_all.at[a], x_fwd.at[a], x_recv.at[a])

    for a in range(p.n_pieces):
        collect_blocks(x_all.at[a], x_recv.at[a])

    gain = gain_ref[...].astype(F32)

    def inverse_spread(block):
        total = 0.0
        for a in range(p.n_pieces):
            v = x_all[a, block].astype(F32)
            total = total + jnp.sum(v * v, axis=-1, keepdims=True)
        return lax.rsqrt(total / p.width + 1e-06)

    def norm_body(k, _):
        for i in range(p.batch):
            block = k * p.batch + i
            inv = inverse_spread(block)
            low = i * p.rows
            for a in range(p.n_pieces):
                v = x_all[a, block].astype(F32) * inv * gain[:, a * p.piece:(a + 1) * p.piece]
                stage[low:low + p.rows, a * p.piece:(a + 1) * p.piece] = v[:p.rows]
            stage[low:low + p.rows, p.width:] = hot_all[block].astype(F32)[:p.rows]
        height = p.batch * p.rows
        at = pl.ds(pl.multiple_of(k * height, height), height)
        normed[at, :] = stage[:, :p.width].astype(BF16)
        hot_rows[at, :] = stage[:, p.width:]
        return 0

    lax.fori_loop(0, p.n_ep // p.batch, norm_body, 0)

    def gates_of(rows):
        return jax.nn.sigmoid(jnp.dot(rows, router_ref[...], preferred_element_type=F32))

    n_ids = router_ref.shape[1]
    gates = gates_of(normed[...])
    lane = lax.broadcasted_iota(jnp.int32, (p.total, n_ids), 1)
    coef = jnp.sum(jnp.where(lane == ep, gates * hot_rows[...][:, :n_ids], 0.0), axis=-1, keepdims=True)

    def hidden_of(w_gate, w_up):
        g = jnp.dot(normed[...], w_gate, preferred_element_type=F32)
        u = jnp.dot(normed[...], w_up, preferred_element_type=F32)
        return g * jax.nn.sigmoid(g) * u

    loads["dg"].wait()
    loads["du"].wait()
    hid_d[...] = hidden_of(dg[...], du[...]).astype(BF16)
    for j in range(p.f_expert // p.e_step):
        loads["eg", j].wait()
        loads["eu", j].wait()
        cols = slice(j * p.e_step, (j + 1) * p.e_step)
        hid_e[:, cols] = (hidden_of(eg[:, cols], eu[:, cols]) * coef).astype(BF16)

    for c in range(p.chunks):
        loads["dd", c].wait()
        loads["ed", c].wait()
        cols = slice(c * p.n_out, (c + 1) * p.n_out)
        value = jnp.dot(hid_e[...], ed[:, cols], preferred_element_type=F32)
        value += jnp.dot(hid_d[...], dd[:, cols], preferred_element_type=F32)
        part[c] = value.astype(BF16)
        for dt in range(p.n_tp):
            for k in range(0 if dt else 1, p.planes):
                column = lax.rem(q + k, p.planes)
                at = pl.ds(pl.multiple_of(column * p.column, p.column), p.column)
                send(part.at[c, at], recv1.at[c, dt * p.planes + k - 1], r1_send, r1_recv.at[c],
                     section, plane_peer(k), lax.rem(tp + dt, p.n_tp))

    inv = inverse_spread(mine)
    for a in range(p.n_pieces):
        cols = slice(a * p.piece, (a + 1) * p.piece)
        own_normed[:, cols] = (x_all[a, mine].astype(F32) * inv * gain[:, cols]).astype(BF16)
    own_gates = gates_of(own_normed[...])
    own_lane = lax.broadcasted_iota(jnp.int32, own_gates.shape, 1)
    own_hot = hot_ref[...].astype(F32)[:, :n_ids]
    zero_share = jnp.sum(jnp.where(own_lane >= p.n_ep, own_gates * own_hot, 0.0), axis=-1, keepdims=True)

    own_rows = pl.ds(pl.multiple_of(q * p.column, p.column), p.column)
    for c in range(p.chunks):
        acc = part[c, own_rows].astype(F32)
        if p.peers:
            arrived(recv1.at[c], r1_recv.at[c])
            for k in range(p.peers):
                acc += recv1[c, k].astype(F32)
        colf[...] = acc
        for i in range(p.depth):
            s2[c, i, :p.rows] = colf[i * p.rows:(i + 1) * p.rows].astype(BF16)
        for i in range(1, p.depth):
            send(s2.at[c, lax.rem(z + i, p.depth)], recv2.at[c, i - 1], r2_send, r2_recv.at[c],
                 section, z_peer(i), tp)

    for c in range(p.chunks):
        a, inner = c // p.per_piece, c % p.per_piece
        cols = slice(inner * p.n_out, (inner + 1) * p.n_out)
        acc = s2[c, z].astype(F32)
        arrived(recv2.at[c], r2_recv.at[c])
        for k in range(p.depth - 1):
            acc += recv2[c, k].astype(F32)
        acc += x_all[a, mine, :, cols].astype(F32)
        acc += zero_share * own_normed[:, c * p.n_out:(c + 1) * p.n_out].astype(F32)
        out_ref[a, :, cols] = acc.astype(BF16)
        if inner == p.per_piece - 1:
            @pl.when(section < p.n_pp - 1)
            def _():
                scatter_block(out_ref.at[a], x_all.at[a], x_send.at[p.n_pieces + a], x_recv.at[a],
                              section + 1, True)

    arrived(hot_all.at[pl.ds(0, n_own)], h_send)
    arrived(hot_all.at[pl.ds(0, n_fwd)], h_fwd)
    for a in range(p.n_pieces):
        arrived(x_all.at[a, pl.ds(0, n_fwd)], x_fwd.at[a])
    if p.peers:
        arrived(recv1, r1_send)
    arrived(recv2, r2_send)

    @pl.when(section == 0)
    def _():
        for a in range(p.n_pieces):
            arrived(x_all.at[a, pl.ds(0, n_own)], x_send.at[a])

    @pl.when(section < p.n_pp - 1)
    def _():
        for a in range(p.n_pieces):
            arrived(x_all.at[a, pl.ds(0, n_own + 1)], x_send.at[p.n_pieces + a])


def on_device(sizes, acts, route_ids, norm_gain, router, dense_gate, dense_up, dense_down,
              expert_gate, expert_up, expert_down):
    n_pp, n_ep, n_tp = sizes
    n_micro, per_group, width = acts.shape
    rows = n_micro * per_group
    f_expert, f_dense = expert_gate.shape[-1], dense_gate.shape[-1]
    p = Plan(n_pp, n_ep, n_tp, rows, width, f_expert, f_dense)
    n_ids = router.shape[-1]
    lanes = -(-n_ids // 128) * 128

    x = jnp.pad(acts.reshape(rows, width), ((0, p.padded - rows), (0, 0)))
    x = x.reshape(p.padded, p.n_pieces, p.piece).transpose(1, 0, 2)
    ids = route_ids[0].reshape(rows, -1)
    hot = jnp.sum((ids[:, :, None] == jnp.arange(lanes, dtype=jnp.int32)).astype(F32), axis=1).astype(BF16)
    hot = jnp.pad(hot, ((0, p.padded - rows), (0, 0)))

    vmem = pl.BlockSpec(memory_space=pltpu.VMEM)
    hbm = pl.BlockSpec(memory_space=pl.ANY)
    dma = pltpu.SemaphoreType.DMA
    n_loads = 2 + 2 * (f_expert // p.e_step) + 2 * p.chunks
    out = pl.pallas_call(
        functools.partial(main_kernel, p),
        out_shape=jax.ShapeDtypeStruct((p.n_pieces, p.padded, p.piece), BF16),
        in_specs=[vmem] * 4 + [hbm] * 6,
        out_specs=vmem,
        scratch_shapes=[
            pltpu.VMEM((p.n_pieces, n_ep, p.padded, p.piece), BF16),
            pltpu.VMEM((n_ep, p.padded, lanes), BF16),
            pltpu.VMEM((p.total, width), BF16),
            pltpu.VMEM((p.total, lanes), F32),
            pltpu.VMEM((p.batch * rows, width + lanes), F32),
            pltpu.VMEM((width, f_dense), BF16),
            pltpu.VMEM((width, f_dense), BF16),
            pltpu.VMEM((f_dense, width), BF16),
            pltpu.VMEM((width, f_expert), BF16),
            pltpu.VMEM((width, f_expert), BF16),
            pltpu.VMEM((f_expert, width), BF16),
            pltpu.VMEM((p.total, f_dense), BF16),
            pltpu.VMEM((p.total, f_expert), BF16),
            pltpu.VMEM((p.chunks, p.total, p.n_out), BF16),
            pltpu.VMEM((p.chunks, max(p.peers, 1), p.column, p.n_out), BF16),
            pltpu.VMEM((p.chunks, p.depth, p.padded, p.n_out), BF16),
            pltpu.VMEM((p.chunks, p.depth - 1, p.padded, p.n_out), BF16),
            pltpu.VMEM((p.column, p.n_out), F32),
            pltpu.VMEM((p.padded, width), BF16),
            dma((n_loads,)),
            dma((2 * p.n_pieces,)),
            dma((p.n_pieces,)),
            dma((p.n_pieces, n_ep)),
            dma, dma, dma((n_ep,)),
            dma, dma((p.chunks,)),
            dma, dma((p.chunks,)),
        ],
        compiler_params=pltpu.CompilerParams(
            collective_id=0, has_side_effects=True, vmem_limit_bytes=60 * 1024 * 1024),
    )(x, hot, norm_gain, router[0], dense_gate[0], dense_up[0], dense_down[0],
      expert_gate[0, 0], expert_up[0, 0], expert_down[0, 0])
    out = out.transpose(1, 0, 2).reshape(p.padded, width)[:rows]
    return out.reshape(1, n_micro, per_group, width)


def solution(mesh):
    sizes = (mesh.shape["pp"], mesh.shape["ep"], mesh.shape["tp"])
    return jax.shard_map(
        functools.partial(on_device, sizes),
        mesh=mesh,
        in_specs=(
            P(None, "ep", None),
            P("pp", None, "ep", None),
            P("pp", None),
            P("pp", None, None),
            P("pp", None, ("ep", "tp")),
            P("pp", None, ("ep", "tp")),
            P("pp", ("ep", "tp"), None),
            P("pp", "ep", None, "tp"),
            P("pp", "ep", None, "tp"),
            P("pp", "ep", "tp", None),
        ),
        out_specs=P("pp", None, "ep", None),
        check_vma=False,
    )
```

time: 464 us -> 76.8 us (0.17)
  the two profiles are of different devices: /device:TPU:0 before, /device:TPU:1 now
where the time goes in v1:
time: 76.8 us; the launch traced here: 76.5 us
  Pallas kernels  69.7 us (91%)
  local copies, waits for them, and re-layouts  6.69 us (9%)
    pallas_call x1, Pallas kernels, on_device(): pl.pallas_call(functools.partial(main_kernel, p), out_shape=jax.ShapeDtyp...  69.7 us
    unnamed x2, local copies, waits for them, and re-layouts  2.97 us

profile of v1, /device:TPU:1, one launch (start us, length us, event | category | flops | bytes accessed | tf_op | source)
XLA Modules:
  0.0 76.5 jit_solution(14798303440403435779)
XLA Ops:
  0.0 0.7 copy.28
  0.7 0.1 convert_reduce_fusion
  0.8 0.6 pad.9.hot_ref
  1.4 0.9 %copy.21 = bf16[2,6,3072]{2,1,0:T(8,128)(2,1)S(1)} copy(bf16[2,6,3072]{2,0,1:T(2,128)(2,1)} %param.10) | data formatting | bytes 147456 | tf_op args[0]
  2.4 0.6 copy.32
  3.0 2.1 %copy.25 = bf16[1,3072,24]{2,1,0:T(8,128)(2,1)} copy(bf16[1,3072,24]{1,2,0:T(8,128)(2,1)} %param.13) | data formatting | bytes 294912 | tf_op args[3]
  5.1 69.7 %shard_map.100 = bf16[2,16,1536]{2,1,0:T(8,128)(2,1)} custom-call(bf16[2,16,1536]{2,1,0:T(8,128)(2,1)} %bitcast.23, bf16[16,128]{1,0:T(8,128)(2,1)} %pad.9.hot_ref, bf16[1,3072]{1,0:T(2,128)(2,1)} %gain_ref.1, bf16[3072,24]{1,0:T(8,128)(2,1)} %bitcast.19, bf16[3072,384]{1,0:T(8,128)(2,1)} %bitcast.20, bf16[3072,384]{1,0:T(8,128)(2,1)} %bitcast.21, ...), custom_call_target="tpu_custom_call" | custom-call | tf_op jit(solution)/shard_map/pallas_call | solution.py:287
  74.8 1.0 %copy.26 = bf16[12,2,1536]{2,1,0:T(2,128)(2,1)S(1)} copy(bf16[12,2,1536]{2,0,1:T(8,128)(2,1)} %bitcast.24) | data formatting | bytes 147456 | tf_op jit(solution)/shard_map/slice | solution.py:324
  75.8 0.1 reshape.15
  75.8 0.7 copy.27
  (3 shorter events, 0.0 us)

commit v2 on v1

--- a/solution.py
+++ b/solution.py
@@ -31,19 +31,23 @@
         self.total = n_ep * rows
         self.column = self.depth * rows
         self.f_expert, self.f_dense = f_expert, f_dense
-        self.n_pieces = 2 if width % 256 == 0 else 1
-        self.piece = width // self.n_pieces
-        self.n_out = divisor_at_most(self.piece, 128, 512)
+        self.n_out = divisor_at_most(width, 128, 512)
         self.chunks = width // self.n_out
-        self.per_piece = self.piece // self.n_out
+        spare = self.padded - rows
+        self.tails = rows // spare if spare and rows % spare == 0 else 0
+        self.spare = spare
+        if self.n_out % (128 * (self.tails + 1)):
+            self.tails = 0
+        self.tail = self.n_out // (self.tails + 1) if self.tails else 0
+        self.main = self.n_out - self.tail
         self.e_step = divisor_at_most(f_expert, 128, 256)
         self.batch = 4 if n_ep % 4 == 0 else 1
         self.peers = self.planes * n_tp - 1
 
 
-def main_kernel(p, x_ref, hot_ref, gain_ref, router_ref, dg_hbm, du_hbm, dd_hbm, eg_hbm, eu_hbm, ed_hbm,
+def main_kernel(p, x_ref, ids_ref, gain_ref, router_ref, dg_hbm, du_hbm, dd_hbm, eg_hbm, eu_hbm, ed_hbm,
                 out_ref, x_all, hot_all, normed, hot_rows, stage, dg, du, dd, eg, eu, ed, hid_d, hid_e,
-                part, recv1, s2, recv2, colf, own_normed, w_sem, x_send, x_fwd, x_recv, h_send, h_fwd, h_recv,
+                part, recv1, s2, recv2, colf, own_normed, own_x, own_hot, tile, packed, x_own, x_next, hot_own, w_sem, x_send, x_fwd, x_recv, h_send, h_fwd, h_recv,
                 r1_send, r1_recv, r2_send, r2_recv):
     section = lax.axis_index("pp")
     ep = lax.axis_index("ep")
@@ -66,6 +70,44 @@
         loads[name] = pltpu.make_async_copy(src, dst, w_sem.at[i])
         loads[name].start()
 
+    micro = x_ref.shape[1]
+    n_ids = router_ref.shape[0]
+
+    def unpack(block, dst, low):
+        for c in range(p.chunks):
+            v = x_all[c, block].astype(F32)
+            left = c * p.n_out
+            dst[low:low + p.rows, left:left + p.main] = v[:p.rows]
+            for j in range(p.tails):
+                dst[low + j * p.spare:low + (j + 1) * p.spare, left + p.main:left + p.n_out] = (
+                    v[p.rows:, j * p.tail:(j + 1) * p.tail])
+
+    def pack(src, left, c, dst):
+        packed[:p.rows, :] = src[:p.rows, left:left + p.main]
+        for j in range(p.tails):
+            packed[p.rows:, j * p.tail:(j + 1) * p.tail] = (
+                src[j * p.spare:(j + 1) * p.spare, left + p.main:left + p.n_out])
+        dst[c] = packed[...].astype(BF16)
+
+    own_x[...] = jnp.zeros_like(own_x)
+    own_hot[...] = jnp.zeros_like(own_hot)
+    packed[...] = jnp.zeros_like(packed)
+    for t in range(x_ref.shape[0]):
+        low = t * micro
+        own_x[low:low + micro, :] = x_ref[t].astype(F32)
+        ids = ids_ref[t]
+        lanes = lax.broadcasted_iota(jnp.int32, (micro, own_hot.shape[1]), 1)
+        named = jnp.zeros(lanes.shape, F32)
+        for k in range(ids.shape[1]):
+            named += (ids[:, k:k + 1] == lanes).astype(F32)
+        own_hot[low:low + micro, :] = named
+    hot_own[...] = own_hot[...].astype(BF16)
+
+    @pl.when(section == 0)
+    def _():
+        for c in range(p.chunks):
+            pack(own_x, c * p.n_out, c, x_own)
+
     def z_peer(i):
         return lax.rem(z + i, p.depth) * p.planes + q
 
@@ -96,40 +138,40 @@
 
     def scatter_block(src, buf, send_sem, recv_sem, to_section, include_self):
         for i in range(1, p.depth):
-            send(src, buf.at[mine], send_sem, recv_sem.at[mine], to_section, z_peer(i), tp)
-        for i in range(0 if include_self else 1, p.planes):
-            send(src, buf.at[mine], send_sem, recv_sem.at[mine], to_section, plane_peer(i), tp)
+            send(src, buf.at[mine], send_sem, recv_sem.at[z], to_section, z_peer(i), tp)
+        for i in range(1, p.planes):
+            send(src, buf.at[mine], send_sem, recv_sem.at[p.depth], to_section, plane_peer(i), tp)
+        if include_self:
+            send(src, buf.at[mine], send_sem, recv_sem.at[z], to_section, ep, tp)
 
     def forward_blocks(buf, fwd_sem, recv_sem):
         for i in range(1, p.depth):
-            block = q * p.depth + lax.rem(z + i, p.depth)
-            arrived(buf.at[block], recv_sem.at[block])
+            source = lax.rem(z + i, p.depth)
+            block = q * p.depth + source
+            arrived(buf.at[block], recv_sem.at[source])
             for k in range(1, p.planes):
-                send(buf.at[block], buf.at[block], fwd_sem, recv_sem.at[block], section, plane_peer(k), tp)
+                send(buf.at[block], buf.at[block], fwd_sem, recv_sem.at[p.depth], section, plane_peer(k), tp)
 
     def collect_blocks(buf, recv_sem):
-        for k in range(1, p.planes):
-            column = lax.rem(q + k, p.planes)
-            for i in range(p.depth):
-                block = column * p.depth + i
-                arrived(buf.at[block], recv_sem.at[block])
+        if p.planes > 1:
+            arrived(buf.at[pl.ds(0, (p.planes - 1) * p.depth)], recv_sem.at[p.depth])
 
     n_own = p.depth - 1 + p.planes - 1
     n_fwd = (p.depth - 1) * (p.planes - 1)
 
     @pl.when(section == 0)
     def _():
-        for a in range(p.n_pieces):
-            scatter_block(x_ref.at[a], x_all.at[a], x_send.at[a], x_recv.at[a], section, False)
-            x_all[a, mine] = x_ref[a]
-
-    scatter_block(hot_ref, hot_all, h_send, h_recv, section, False)
-    hot_all[mine] = hot_ref[...]
+        for a in range(p.chunks):
+            scatter_block(x_own.at[a], x_all.at[a], x_send.at[a], x_recv.at[a], section, False)
+            x_all[a, mine] = x_own[a]
+
+    scatter_block(hot_own, hot_all, h_send, h_recv, section, False)
+    hot_all[mine] = hot_own[...]
     s2[...] = jnp.zeros_like(s2)
 
     @pl.when(section == 0)
     def _():
-        for a in range(p.n_pieces):
+        for a in range(p.chunks):
             forward_blocks(x_all.at[a], x_fwd.at[a], x_recv.at[a])
 
     forward_blocks(hot_all, h_fwd, h_recv)
@@ -137,43 +179,37 @@
 
     @pl.when(section > 0)
     def _():
-        for a in range(p.n_pieces):
-            arrived(x_all.at[a, mine], x_recv.at[a, mine])
+        for a in range(p.chunks):
+            arrived(x_all.at[a, mine], x_recv.at[a, z])
             forward_blocks(x_all.at[a], x_fwd.at[a], x_recv.at[a])
 
-    for a in range(p.n_pieces):
+    for a in range(p.chunks):
         collect_blocks(x_all.at[a], x_recv.at[a])
 
     gain = gain_ref[...].astype(F32)
 
-    def inverse_spread(block):
-        total = 0.0
-        for a in range(p.n_pieces):
-            v = x_all[a, block].astype(F32)
-            total = total + jnp.sum(v * v, axis=-1, keepdims=True)
-        return lax.rsqrt(total / p.width + 1e-06)
+    def rms_normed(v):
+        spread = jnp.mean(v * v, axis=-1, keepdims=True)
+        return (v * lax.rsqrt(spread + 1e-06) * gain).astype(BF16)
 
     def norm_body(k, _):
         for i in range(p.batch):
             block = k * p.batch + i
-            inv = inverse_spread(block)
             low = i * p.rows
-            for a in range(p.n_pieces):
-                v = x_all[a, block].astype(F32) * inv * gain[:, a * p.piece:(a + 1) * p.piece]
-                stage[low:low + p.rows, a * p.piece:(a + 1) * p.piece] = v[:p.rows]
+            unpack(block, stage, low)
             stage[low:low + p.rows, p.width:] = hot_all[block].astype(F32)[:p.rows]
         height = p.batch * p.rows
         at = pl.ds(pl.multiple_of(k * height, height), height)
-        normed[at, :] = stage[:, :p.width].astype(BF16)
+        normed[at, :] = rms_normed(stage[:, :p.width])
         hot_rows[at, :] = stage[:, p.width:]
         return 0
 
     lax.fori_loop(0, p.n_ep // p.batch, norm_body, 0)
 
     def gates_of(rows):
-        return jax.nn.sigmoid(jnp.dot(rows, router_ref[...], preferred_element_type=F32))
-
-    n_ids = router_ref.shape[1]
+        return jax.nn.sigmoid(lax.dot_general(
+            rows, router_ref[...], (((1,), (1,)), ((), ())), preferred_element_type=F32))
+
     gates = gates_of(normed[...])
     lane = lax.broadcasted_iota(jnp.int32, (p.total, n_ids), 1)
     coef = jnp.sum(jnp.where(lane == ep, gates * hot_rows[...][:, :n_ids], 0.0), axis=-1, keepdims=True)
@@ -206,14 +242,12 @@
                 send(part.at[c, at], recv1.at[c, dt * p.planes + k - 1], r1_send, r1_recv.at[c],
                      section, plane_peer(k), lax.rem(tp + dt, p.n_tp))
 
-    inv = inverse_spread(mine)
-    for a in range(p.n_pieces):
-        cols = slice(a * p.piece, (a + 1) * p.piece)
-        own_normed[:, cols] = (x_all[a, mine].astype(F32) * inv * gain[:, cols]).astype(BF16)
+    unpack(mine, own_x, 0)
+    own_normed[...] = rms_normed(own_x[...])
     own_gates = gates_of(own_normed[...])
     own_lane = lax.broadcasted_iota(jnp.int32, own_gates.shape, 1)
-    own_hot = hot_ref[...].astype(F32)[:, :n_ids]
-    zero_share = jnp.sum(jnp.where(own_lane >= p.n_ep, own_gates * own_hot, 0.0), axis=-1, keepdims=True)
+    own_named = own_hot[...][:, :n_ids]
+    zero_share = jnp.sum(jnp.where(own_lane >= p.n_ep, own_gates * own_named, 0.0), axis=-1, keepdims=True)
 
     own_rows = pl.ds(pl.multiple_of(q * p.column, p.column), p.column)
     for c in range(p.chunks):
@@ -230,24 +264,26 @@
                  section, z_peer(i), tp)
 
     for c in range(p.chunks):
-        a, inner = c // p.per_piece, c % p.per_piece
-        cols = slice(inner * p.n_out, (inner + 1) * p.n_out)
+        cols = slice(c * p.n_out, (c + 1) * p.n_out)
         acc = s2[c, z].astype(F32)
         arrived(recv2.at[c], r2_recv.at[c])
         for k in range(p.depth - 1):
             acc += recv2[c, k].astype(F32)
-        acc += x_all[a, mine, :, cols].astype(F32)
-        acc += zero_share * own_normed[:, c * p.n_out:(c + 1) * p.n_out].astype(F32)
-        out_ref[a, :, cols] = acc.astype(BF16)
-        if inner == p.per_piece - 1:
+        acc += own_x[:, cols]
+        acc += zero_share * own_normed[:, cols].astype(F32)
+        tile[...] = acc
+        if p.n_pp > 1:
             @pl.when(section < p.n_pp - 1)
             def _():
-                scatter_block(out_ref.at[a], x_all.at[a], x_send.at[p.n_pieces + a], x_recv.at[a],
+                pack(tile, 0, c, x_next)
+                scatter_block(x_next.at[c], x_all.at[c], x_send.at[p.chunks + c], x_recv.at[c],
                               section + 1, True)
+        for t in range(x_ref.shape[0]):
+            out_ref[t, :, cols] = tile[t * micro:(t + 1) * micro, :].astype(BF16)
 
     arrived(hot_all.at[pl.ds(0, n_own)], h_send)
     arrived(hot_all.at[pl.ds(0, n_fwd)], h_fwd)
-    for a in range(p.n_pieces):
+    for a in range(p.chunks):
         arrived(x_all.at[a, pl.ds(0, n_fwd)], x_fwd.at[a])
     if p.peers:
         arrived(recv1, r1_send)
@@ -255,13 +291,13 @@
 
     @pl.when(section == 0)
     def _():
-        for a in range(p.n_pieces):
+        for a in range(p.chunks):
             arrived(x_all.at[a, pl.ds(0, n_own)], x_send.at[a])
 
     @pl.when(section < p.n_pp - 1)
     def _():
-        for a in range(p.n_pieces):
-            arrived(x_all.at[a, pl.ds(0, n_own + 1)], x_send.at[p.n_pieces + a])
+        for a in range(p.chunks):
+            arrived(x_all.at[a, pl.ds(0, n_own + 1)], x_send.at[p.chunks + a])
 
 
 def on_device(sizes, acts, route_ids, norm_gain, router, dense_gate, dense_up, dense_down,
@@ -274,11 +310,8 @@
     n_ids = router.shape[-1]
     lanes = -(-n_ids // 128) * 128
 
-    x = jnp.pad(acts.reshape(rows, width), ((0, p.padded - rows), (0, 0)))
-    x = x.reshape(p.padded, p.n_pieces, p.piece).transpose(1, 0, 2)
-    ids = route_ids[0].reshape(rows, -1)
-    hot = jnp.sum((ids[:, :, None] == jnp.arange(lanes, dtype=jnp.int32)).astype(F32), axis=1).astype(BF16)
-    hot = jnp.pad(hot, ((0, p.padded - rows), (0, 0)))
+    x = acts.transpose(1, 0, 2)
+    ids = route_ids[0].transpose(1, 0, 2)
 
     vmem = pl.BlockSpec(memory_space=pltpu.VMEM)
     hbm = pl.BlockSpec(memory_space=pl.ANY)
@@ -286,11 +319,11 @@
     n_loads = 2 + 2 * (f_expert // p.e_step) + 2 * p.chunks
     out = pl.pallas_call(
         functools.partial(main_kernel, p),
-        out_shape=jax.ShapeDtypeStruct((p.n_pieces, p.padded, p.piece), BF16),
+        out_shape=jax.ShapeDtypeStruct((per_group, n_micro, width), BF16),
         in_specs=[vmem] * 4 + [hbm] * 6,
         out_specs=vmem,
         scratch_shapes=[
-            pltpu.VMEM((p.n_pieces, n_ep, p.padded, p.piece), BF16),
+            pltpu.VMEM((p.chunks, n_ep, p.padded, p.main), BF16),
             pltpu.VMEM((n_ep, p.padded, lanes), BF16),
             pltpu.VMEM((p.total, width), BF16),
             pltpu.VMEM((p.total, lanes), F32),
@@ -309,20 +342,26 @@
             pltpu.VMEM((p.chunks, p.depth - 1, p.padded, p.n_out), BF16),
             pltpu.VMEM((p.column, p.n_out), F32),
             pltpu.VMEM((p.padded, width), BF16),
+            pltpu.VMEM((p.padded, width), F32),
+            pltpu.VMEM((p.padded, lanes), F32),
+            pltpu.VMEM((p.padded, p.n_out), F32),
+            pltpu.VMEM((p.padded, p.main), F32),
+            pltpu.VMEM((p.chunks, p.padded, p.main), BF16),
+            pltpu.VMEM((p.chunks, p.padded, p.main), BF16),
+            pltpu.VMEM((p.padded, lanes), BF16),
             dma((n_loads,)),
-            dma((2 * p.n_pieces,)),
-            dma((p.n_pieces,)),
-            dma((p.n_pieces, n_ep)),
-            dma, dma, dma((n_ep,)),
+            dma((2 * p.chunks,)),
+            dma((p.chunks,)),
+            dma((p.chunks, p.depth + 1)),
+            dma, dma, dma((p.depth + 1,)),
             dma, dma((p.chunks,)),
             dma, dma((p.chunks,)),
         ],
         compiler_params=pltpu.CompilerParams(
             collective_id=0, has_side_effects=True, vmem_limit_bytes=60 * 1024 * 1024),
-    )(x, hot, norm_gain, router[0], dense_gate[0], dense_up[0], dense_down[0],
+    )(x, ids, norm_gain, router[0].T, dense_gate[0], dense_up[0], dense_down[0],
       expert_gate[0, 0], expert_up[0, 0], expert_down[0, 0])
-    out = out.transpose(1, 0, 2).reshape(p.padded, width)[:rows]
-    return out.reshape(1, n_micro, per_group, width)
+    return out.transpose(1, 0, 2)[None]
 
 
 def solution(mesh):

time: 76.8 us -> 65.8 us (0.86)
  Pallas kernels: 69.7 us -> 64 us
  local copies, waits for them, and re-layouts: 6.69 us -> 1.57 us
    pallas_call x1, Pallas kernels: 69.7 us -> 64 us  [on_device(): pl.pallas_call(functools.partial(main_kernel, p), out_shape=jax.ShapeDtyp...]
    reshape x4 -> x0, local copies, waits for them, and re-layouts: 1.43 us -> none  [the longest x2 0.76 us: on_device(): return out.reshape(1, n_micro, per_group, width)]
    unnamed x2 -> x1, local copies, waits for them, and re-layouts: 2.97 us -> 1.57 us
    slice x1 -> x0, local copies, waits for them, and re-layouts: 0.97 us -> none  [on_device(): out = out.transpose(1, 0, 2).reshape(p.padded, width)[:rows]]
where the time goes in v2:
time: 65.8 us; the launch traced here: 65.6 us
  Pallas kernels  64 us (97%)
  local copies, waits for them, and re-layouts  1.57 us (2%)
    pallas_call x1, Pallas kernels, on_device(): pl.pallas_call(functools.partial(main_kernel, p), out_shape=jax.ShapeDtyp...  64 us
    unnamed x1, local copies, waits for them, and re-layouts  1.57 us

profile of v2, /device:TPU:1, one launch (start us, length us, event | category | flops | bytes accessed | tf_op | source)
XLA Modules:
  0.0 65.6 jit_solution(13814070255051423529)
XLA Ops:
  0.0 64.0 %shard_map.100 = bf16[6,2,3072]{2,1,0:T(2,128)(2,1)} custom-call(bf16[6,2,3072]{2,1,0:T(2,128)(2,1)} %bitcast.24, s32[6,2,8]{2,1,0:T(2,128)} %bitcast.25, bf16[1,3072]{1,0:T(2,128)(2,1)} %gain_ref.1, bf16[24,3072]{1,0:T(8,128)(2,1)} %bitcast.23, bf16[3072,384]{1,0:T(8,128)(2,1)} %bitcast.19, bf16[3072,384]{1,0:T(8,128)(2,1)} %bitcast.20, ...), custom_call_target="tpu_custom_call" | custom-call | tf_op jit(solution)/shard_map/pallas_call | solution.py:320
  64.0 1.6 %copy.12 = bf16[1,2,6,3072]{3,1,2,0:T(2,128)(2,1)} copy(bf16[1,2,6,3072]{3,1,2,0:T(2,128)(2,1)} %bitcast.22) | data formatting | bytes 147456
